TPU v7x, 256 devices: a whole 4x4x8 slice. The times are simulated.
256 devices in a mesh: dp: 2 (over core), seq: 32 (over z, x), tensor: 4 (over y).
Axes of the slice: x: 4, y: 4, z: 8, core: 2. Of those that a mesh axis runs over, the one named last changes fastest.
Arguments:
- tokens: bfloat16 [2048, 4, 5120], P('seq', 'dp'), parts along dimension 1, may hold values from -6 to 6
- w_query: bfloat16 [5120, 5120], P(None, 'tensor'), may hold values from -0.5 to 0.5, as said below
- w_key: bfloat16 [5120, 5120], P(None, 'tensor'), may hold values from -0.5 to 0.5, as said below
- w_value: bfloat16 [5120, 5120], P(None, 'tensor'), may hold values from -0.078125 to 0.078125
- w_out: bfloat16 [5120, 5120], P('tensor'), may hold values from -0.125 to 0.125
- gain_query: float32 [5120], P('tensor'), may hold values from 0.5 to 4
- gain_key: float32 [5120], P('tensor'), may hold values from 0.5 to 4
Outputs:
- attended: bfloat16 [2048, 4, 5120], P(('seq', 'tensor'), 'dp'), parts along dimension 1
There are 2 independent parts, one for each index of `dp`. A program takes and returns all parts, laid end to end along the dimension named above; an argument that names none is the same for every part. Nothing has to cross between parts.
Inputs may be any that keep to these rules, and one draw needn't show every extreme that they name: `w_query`: entries of order 5120 ** -0.5 with unequal column scales. `w_key`: entries of order 5120 ** -0.5 with unequal column scales.
All inputs are finite; a program needn't handle non-finite values.
Results may differ from a plain program's by a relative error of at most 0.013.
The roundings to bfloat16 on the way count: a program that leaves them out, or rounds other values in their place, can miss the bound.
Values may be sent and summed in bfloat16 or wider, within the bound.
A program may use at most 256 MiB of HBM per device.

v0:
```python
import jax
import jax.numpy as jnp
from jax import lax
from jax.sharding import PartitionSpec as P

HEADS = 40
HEAD_DIM = 128


def sent_to_all(array, axis):
    copies = jnp.broadcast_to(array, (lax.axis_size(axis), *array.shape))
    return lax.all_to_all(copies, axis, split_axis=0, concat_axis=0, tiled=True)


def of_everyone(array, axis):
    everything = sent_to_all(array, axis)
    return jnp.sum(everything, axis=0)


def together(arrays, axis):
    ravelled, at, outs = (jnp.concatenate([a.reshape(-1) for a in arrays]), 0, [])
    subtotal = of_everyone(ravelled, axis)
    for a in arrays:
        outs.append(subtotal[at : at + a.size].reshape(a.shape))
        at += a.size
    return tuple(outs)


def sent_together(arrays, axis, dim, along):
    ends, at = ([], 0)
    for a in arrays[:-1]:
        at += a.shape[along]
        ends.append(at)
    both = jnp.concatenate(arrays, axis=along)
    return tuple(jnp.split(lax.all_gather(both, axis, axis=dim, tiled=True), ends, axis=along))


def cut_along(array, dim, length):
    lengths = array.shape
    pieces = array.reshape(*lengths[:dim], length, lengths[dim] // length, *lengths[dim + 1 :])
    return jnp.moveaxis(pieces, dim, 0)


def summed_on_arrival(array, axis, dim):
    length = lax.axis_size(axis)
    pieces = lax.all_to_all(cut_along(array, dim, length), axis, 0, 0, tiled=True)
    return jnp.sum(pieces.astype(jnp.float32), axis=0)


def rotary(field, positions):
    half = HEAD_DIM // 2
    shaped = field.reshape(field.shape[0], -1, HEAD_DIM)
    freqs = jnp.exp(-jnp.log(500000.0) * jnp.arange(half, dtype=jnp.float32) * 2.0 / HEAD_DIM)
    angle = positions.astype(jnp.float32)[:, None] * freqs[None, :]
    cosine = jnp.cos(angle)[:, None, :]
    sine = jnp.sin(angle)[:, None, :]
    first = shaped[..., :half]
    second = shaped[..., half:]
    turned = jnp.concatenate(
        [first * cosine - second * sine, second * cosine + first * sine], axis=-1
    )
    return turned.reshape(field.shape[0], -1)


def local(tokens, w_query, w_key, w_value, w_out, gain_query, gain_key):
    tok_rows = tokens.shape[0]
    seq_count = tokens.shape[1]
    local_width = w_query.shape[1]
    local_heads = local_width // HEAD_DIM
    width = HEADS * HEAD_DIM
    flat = tokens.reshape(tok_rows * seq_count, tokens.shape[2])
    query = jnp.dot(flat, w_query, preferred_element_type=jnp.float32)
    key_raw = jnp.dot(flat, w_key, preferred_element_type=jnp.float32)
    sum_query, sum_key = together(
        (jnp.sum(query * query, axis=1), jnp.sum(key_raw * key_raw, axis=1)), "tensor"
    )
    value = jnp.dot(flat, w_value, preferred_element_type=jnp.float32).astype(jnp.bfloat16)
    scale_q = lax.rsqrt(sum_query / width + 1e-06)
    scale_k = lax.rsqrt(sum_key / width + 1e-06)
    my_block = lax.axis_index("seq")
    positions = my_block * tok_rows + jnp.arange(tok_rows, dtype=jnp.int32)
    row_positions = (positions[:, None] + jnp.zeros((1, seq_count), jnp.int32)).reshape(-1)
    q_normed = rotary(query * scale_q[:, None] * gain_query[None, :], row_positions).astype(
        jnp.bfloat16
    )
    k_normed = rotary(key_raw * scale_k[:, None] * gain_key[None, :], row_positions).astype(
        jnp.bfloat16
    )
    q_heads = q_normed.reshape(tok_rows, seq_count, local_heads, HEAD_DIM)
    k_local = k_normed.reshape(tok_rows, seq_count, local_width)
    v_local = value.reshape(tok_rows, seq_count, local_width)
    factor = HEAD_DIM ** (-0.5)

    def update(carry, key_block, value_block, key_pos):
        count = key_block.shape[0]
        key_heads = key_block.reshape(count, seq_count, local_heads, HEAD_DIM)
        value_heads = value_block.reshape(count, seq_count, local_heads, HEAD_DIM)
        scores = (
            jnp.einsum("qshd,kshd->shqk", q_heads, key_heads, preferred_element_type=jnp.float32)
            * factor
        )
        allowed = (key_pos[None, None, None, :] <= positions[None, None, :, None]) & (
            key_pos[None, None, None, :] >= 0
        )
        old_max, old_total, old_acc = carry
        new_max = jnp.maximum(old_max, jnp.max(jnp.where(allowed, scores, -1e30), axis=3))
        expo = jnp.where(allowed, jnp.exp(scores - new_max[..., None]), 0.0)
        new_total = jnp.sum(expo, axis=3)
        added = jnp.einsum(
            "shqk,kshd->shqd",
            expo.astype(jnp.bfloat16),
            value_heads,
            preferred_element_type=jnp.float32,
        )
        return (new_max, new_total, added)

    start_state = (
        jnp.full((seq_count, local_heads, tok_rows), -1e30, jnp.float32),
        jnp.zeros((seq_count, local_heads, tok_rows), jnp.float32),
        jnp.zeros((seq_count, local_heads, tok_rows, HEAD_DIM), jnp.float32),
    )
    piece = sent_together((k_local, v_local), "seq", 0, 1)
    key_pos = jnp.arange(piece[0].shape[0], dtype=jnp.int32)
    final_state = lax.cond(
        jnp.int32(0) > positions[tok_rows - 1],
        lambda state: state,
        lambda state: update(state, piece[0], piece[1], key_pos),
        start_state,
    )
    final_max, final_total, final_acc = final_state
    mixed = (final_acc / final_total[..., None]).astype(jnp.bfloat16)
    mixed = jnp.transpose(mixed, (2, 0, 1, 3)).reshape(tok_rows, seq_count, local_width)
    return summed_on_arrival(
        jnp.dot(mixed, w_out, preferred_element_type=jnp.float32).astype(jnp.bfloat16), "tensor", 0
    ).astype(jnp.bfloat16)


def solution(mesh):
    return jax.shard_map(
        local,
        mesh=mesh,
        in_specs=(
            P("seq", "dp", None),
            P(None, "tensor"),
            P(None, "tensor"),
            P(None, "tensor"),
            P("tensor", None),
            P("tensor"),
            P("tensor"),
        ),
        out_specs=P(("seq", "tensor"), "dp", None),
        check_vma=False,
    )
```

profile of v0, /device:TPU:192, one launch (start us, length us, event | category | flops | bytes accessed | tf_op | source)
XLA Modules:
  0.0 311.5 jit_solution(5106080428587252340)
XLA Ops:
  6.5 3.1 reshape.164
  9.7 6.8 %multiply_reduce_fusion.1 = (f32[128]{0:T(128)S(1)}, f32[128,1280]{1,0:T(8,128)S(1)}) fusion(bf16[128,5120]{1,0:T(8,128)(2,1)S(1)} %reshape.164, bf16[5120,1280]{1,0:T(8,128)(2,1)} %param.10), kind=kOutput, calls=%fused_computation.26 | convolution fusion | flops 1678049152 | bytes 15073792 | tf_op jit(solution)/shard_map/dot_general | solution.py:72
  16.5 1.6 copy-done
  18.1 2.0 multiply_reduce_fusion
  20.1 0.6 broadcast_in_dim.26
  20.7 4.5 %all-to-all-start = ((f32[4,1,256]{2,1,0:T(1,128)}), f32[4,1,256]{2,1,0:T(1,128)S(1)}, u32[]{:S(2)}, u32[]{:S(2)}) async-start(f32[4,1,256]{2,1,0:T(1,128)} %broadcast_in_dim.26), calls=%async_computation | async-start | bytes 8192 | tf_op jit(solution)/shard_map/all_to_all | solution.py:12
  25.4 6.6 %convolution_convert_fusion = bf16[128,1280]{1,0:T(8,128)(2,1)S(1)} fusion(bf16[128,5120]{1,0:T(8,128)(2,1)S(1)} %reshape.164, bf16[5120,1280]{1,0:T(8,128)(2,1)} %param.12), kind=kOutput, calls=%fused_computation.19 | convolution fusion | flops 1677885440 | bytes 14745600 | tf_op jit(solution)/shard_map/dot_general | solution.py:77
  32.2 0.8 reshape.167
  33.3 0.2 copy.47
  33.7 0.4 copy.48
  34.3 2.5 pad_maximum_fusion.1
  36.8 0.6 slice.21
  38.5 158.7 %all-gather.2.cloned.1.call-done = bf16[2048,4,1280]{2,1,0:T(4,128)(2,1)} async-done(((bf16[64,4,1280]{2,1,0:T(4,128)(2,1)}), bf16[2048,4,1280]{2,1,0:T(4,128)(2,1)}) %all-gather.2.cloned.1.call-update) | async-done | bytes 20971536 | tf_op jit(solution)/shard_map/all_gather | solution.py:35
  197.2 78.1 %conditional.1 = (f32[2,10,64]{2,1,0:T(8,128)S(1)}, f32[2,10,64,128]{3,2,1,0:T(8,128)S(1)}) conditional(s32[]{:T(128)} %bitcast.3, (s32[2048]{0:T(1024)S(1)}, s32[64]{0:T(128)S(1)}, s32[2048]{0:T(1024)S(1)}, bf16[128,10,128]{0,2,1:T(8,128)(2,1)S(1)}, bf16[2048,4,1280]{2,1,0:T(4,128)(2,1)}) %tuple.13, () %tuple.14), branch_computations={%region_3.6_spmd, %region_6.7_spmd} | conditional | flops 1371276032 | bytes 138529040 | solution.py:124
  197.2 32.5 %copy.50 = bf16[2048,4,1280]{0,2,1:T(8,128)(2,1)} copy(bf16[2048,4,1280]{2,1,0:T(4,128)(2,1)} %get-tuple-element.47) | data formatting | bytes 41943040 | tf_op jit(solution)/shard_map
  229.6 16.5 %fusion.21 = (bf16[2048,2,1280]{0,2,1:T(8,128)(2,1)}, bf16[2048,2,1280]{0,2,1:T(8,128)(2,1)}) fusion(bf16[2048,4,1280]{0,2,1:T(8,128)(2,1)} %copy.50), kind=kLoop, calls=%fused_computation.43 | loop fusion | bytes 41943040 | tf_op jit(solution)/shard_map/split | solution.py:35
  246.3 0.4 copy.49
  246.7 11.2 %select_reduce_fusion = (f32[2,10,64]{2,1,0:T(8,128)S(1)}, f32[2,10,64,2048]{3,2,1,0:T(8,128)}) fusion(pred[64,2048]{1,0:T(8,128)(4,1)S(1)} %compare_and_fusion, bf16[2048,2,10,128]{0,3,2,1:T(8,128)(2,1)} %bitcast.28, bf16[64,2,10,128]{3,2,1,0:T(8,128)(2,1)S(1)} %bitcast.32), kind=kOutput, calls=%fused_computation.1 | convolution fusion | flops 678951680 | bytes 21435392 | tf_op jit(solution)/shard_map/cond/branch_0_fun/qshd,kshd->shqk/dot_general | solution.py:99
  257.9 10.8 %fusion.2 = f32[2,10,64,128]{3,2,1,0:T(8,128)S(1)} fusion(bf16[2048,2,10,128]{0,3,2,1:T(8,128)(2,1)} %bitcast.29, f32[2,10,64,2048]{3,2,1,0:T(8,128)} %get-tuple-element.51, f32[2,10,64]{2,1,0:T(8,128)S(1)} %broadcast_maximum_fusion, pred[64,2048]{1,0:T(8,128)(4,1)S(1)} %compare_and_fusion), kind=kOutput, calls=%fused_computation.4 | convolution fusion | flops 681574400 | bytes 21763072 | tf_op jit(solution)/shard_map/cond/branch_0_fun/shqk,kshd->shqd/dot_general | solution.py:109
  268.7 6.5 %fusion.1 = f32[2,10,64]{2,1,0:T(8,128)S(1)} fusion(f32[2,10,64,2048]{3,2,1,0:T(8,128)} %get-tuple-element.51, f32[2,10,64]{2,1,0:T(8,128)S(1)} %broadcast_maximum_fusion, pred[64,2048]{1,0:T(8,128)(4,1)S(1)} %compare_and_fusion), kind=kLoop, calls=%fused_computation.3 | loop fusion | flops 10484480 | bytes 10627072 | tf_op jit(solution)/shard_map/cond/branch_0_fun/reduce_sum | solution.py:108
  275.2 6.6 %fusion.14 = bf16[64,2,5120]{2,0,1:T(8,128)(2,1)S(1)} fusion(bf16[1280,5120]{1,0:T(8,128)(2,1)} %param.13, f32[2,10,64,128]{3,2,1,0:T(8,128)S(1)} %get-tuple-element.26, f32[2,10,64]{2,1,0:T(8,128)S(1)} %get-tuple-element.27), kind=kOutput, calls=%fused_computation.18 | convolution fusion | flops 1678704640 | bytes 15078400 | tf_op jit(solution)/shard_map/dot_general | solution.py:134
  282.0 21.3 %all_to_all.11 = bf16[4,16,2,5120]{3,1,2,0:T(8,128)(2,1)S(1)} all-to-all(bf16[4,16,2,5120]{3,1,2,0:T(8,128)(2,1)S(1)} %copy.52), channel_id=1, replica_groups=mesh['dp'=2,'seq'=32,'tensor'=4] {'tensor'}, dimensions={0} | all-to-all | bytes 2621440 | tf_op jit(solution)/shard_map/all_to_all | solution.py:46
  303.2 0.3 reduce_sum.51
  303.5 1.1 copy.54
  (29 shorter events, 1.6 us)
Async XLA Ops:
  9.7 8.5 %copy-start = (bf16[5120,1280]{1,0:T(8,128)(2,1)S(1)}, bf16[5120,1280]{1,0:T(8,128)(2,1)}, u32[]{:S(2)}) copy-start(bf16[5120,1280]{1,0:T(8,128)(2,1)} %param.11) | copy-start | bytes 39321604
  20.7 12.4 %all-to-all-start = ((f32[4,1,256]{2,1,0:T(1,128)}), f32[4,1,256]{2,1,0:T(1,128)S(1)}, u32[]{:S(2)}, u32[]{:S(2)}) async-start(f32[4,1,256]{2,1,0:T(1,128)} %broadcast_in_dim.26), calls=%async_computation | async-start | bytes 8192 | tf_op jit(solution)/shard_map/all_to_all | solution.py:12
  25.1 172.0 %all-gather.2.cloned.1.call-start = ((), (), s32[]{:S(2)}) async-start(), calls=%async_computation.2 | async-start | bytes 21626880 | tf_op jit(solution)/shard_map/all_gather | solution.py:35
  25.4 7.7 %copy-start.1 = (f32[1280]{0:T(1024)S(1)}, f32[1280]{0:T(1024)}, u32[]{:S(2)}) copy-start(f32[1280]{0:T(1024)} %param.15) | copy-start | bytes 15364
  25.4 7.7 %copy-start.2 = (f32[1280]{0:T(1024)S(1)}, f32[1280]{0:T(1024)}, u32[]{:S(2)}) copy-start(f32[1280]{0:T(1024)} %param.14) | copy-start | bytes 15364
Sparse Core Ops, SparseCore 0:
  37.0 160.1 all-gather.1
where the time goes:
time: 316 us; the launch traced here: 311 us
  waiting for transfers between devices  159 us (50%)
  local copies, waits for them, and re-layouts  58.5 us (19%)
  matrix products  44 us (14%)
  blocking collectives  21.3 us (7%)
  between operations  14.2 us (4%)
  other arithmetic  10.2 us (3%)
  starting transfers between devices  4.46 us (1%)
    all_gather x1, waiting for transfers between devices, sent_together(): lax.all_gather(both, axis, axis=dim, tiled=True)  159 us
    another operation x2, local copies, waits for them, and re-layouts  32.9 us
    all_to_all x1, blocking collectives, summed_on_arrival(): lax.all_to_all(cut_along(array, dim, length), axis, 0, 0, tiled=True)  21.3 us
    split x1, local copies, waits for them, and re-layouts, sent_together(): jnp.split(lax.all_gather(both, axis, axis=dim, tiled=True), ends, axis=al...  16.5 us
    dot_general x1, matrix products, update(): jnp.einsum('qshd,kshd->shqk', q_heads, key_heads, preferred_element_type=...  11.2 us
    dot_general x1, matrix products, update(): jnp.einsum('shqk,kshd->shqd', expo.astype(jnp.bfloat16), value_heads, pre...  10.8 us
    dot_general x1, matrix products, local(): query = jnp.dot(flat, w_query, preferred_element_type=jnp.float32)  6.83 us
    dot_general x1, matrix products, local(): jnp.dot(mixed, w_out, preferred_element_type=jnp.float32)  6.65 us
  transfers between devices with their start and end apart: 2, of which 1 were waited for; matrix products, arithmetic and copies ran while one was open for 3% of the time, Pallas kernels for 0%

commit v1 on v0

v1 whole, which is shorter than its diff:
```python
import functools

import jax
import jax.numpy as jnp
import numpy as np
from jax import lax
from jax.experimental import pallas as pl
from jax.experimental.pallas import tpu as pltpu
from jax.sharding import PartitionSpec as P

HEADS = 40
HEAD_DIM = 128
D = 5120
SEQ_DEV = 32
TENSOR = 4
ROWS = 64
PAIR_ROWS = 128
LOCAL = 1280
TILES = 5
WIDE = 256
SLOTS = 4
AHEAD = 3
CHUNK = 512
QB = 256
MESH = pl.DeviceIdType.MESH
F32 = jnp.float32
BF16 = jnp.bfloat16


def pair_device(tile, x):
    z = lax.rem((8 * tile) // 5 + 2 * x, 8)
    return z * 4 + x


def kernel(x_ref, gq_ref, gk_ref, freq_ref, wq_hbm, wk_hbm, wv_hbm, wo_hbm, out_ref,
           wbuf, wobuf, raw, send, recv, amix, mixed, perm, part, osend, orecv, oself,
           ssend, srecv, tabs, wsem, wosem, send_sem, recv_sem, mix_send_sem, mix_sem,
           ss_send_sem, ss_sem, o_send_sem, o_sem):
    me = lax.axis_index("seq")
    t = lax.axis_index("tensor")
    barrier = pltpu.get_barrier_semaphore()

    def greet(d, _):
        pl.semaphore_signal(barrier, inc=1, device_id={"seq": lax.rem(me + d, SEQ_DEV)}, device_id_type=MESH)
        return 0

    lax.fori_loop(1, SEQ_DEV, greet, 0)
    for d in range(1, TENSOR):
        pl.semaphore_signal(barrier, inc=1, device_id={"tensor": lax.rem(t + d, TENSOR)}, device_id_type=MESH)

    weights = (wv_hbm, wk_hbm, wq_hbm)

    def tile_at(s):
        return lax.rem(s + me, TILES)

    def w_copy(mat, s):
        slot = lax.rem(mat * TILES + s, SLOTS)
        cols = pl.ds(pl.multiple_of(tile_at(s) * WIDE, WIDE), WIDE)
        return pltpu.make_async_copy(weights[mat].at[:, cols], wbuf.at[slot], wsem.at[slot])

    for s in range(AHEAD):
        w_copy(0, s).start()

    def prefetch(mat, s):
        later = s + AHEAD

        @pl.when(later < TILES)
        def _():
            w_copy(mat, later).start()

        if mat < 2:
            @pl.when(later >= TILES)
            def _():
                w_copy(mat + 1, later - TILES).start()

    def product(mat, s):
        prefetch(mat, s)
        w_copy(mat, s).wait()
        slot = lax.rem(mat * TILES + s, SLOTS)
        return jnp.dot(x_ref[...], wbuf[slot], preferred_element_type=F32)

    def send_tile(mat, tile, blocks):
        for x in range(4):
            send[mat, tile * 4 + x] = blocks[x]
        for x in range(4):
            dest = pair_device(tile, x)
            src = send.at[mat, tile * 4 + x]
            dst = recv.at[mat, pl.ds(pl.multiple_of(me * ROWS, ROWS), ROWS), :]

            @pl.when(dest != me)
            def _():
                pltpu.make_async_remote_copy(
                    src_ref=src, dst_ref=dst, send_sem=send_sem.at[mat], recv_sem=recv_sem.at[mat],
                    device_id={"seq": dest}, device_id_type=MESH).start()

            @pl.when(dest == me)
            def _():
                pltpu.make_async_copy(src, dst, recv_sem.at[mat]).start()

    lane = lax.broadcasted_iota(jnp.int32, (ROWS, HEAD_DIM), 1)
    pos = lax.broadcasted_iota(jnp.int32, (ROWS, HEAD_DIM), 0) + me * ROWS
    angle = pos.astype(F32) * freq_ref[...]
    sine = jnp.sin(angle)
    tabs[0] = jnp.cos(angle)
    tabs[1] = jnp.where(lane < HEAD_DIM // 2, -sine, sine)

    pl.semaphore_wait(barrier, SEQ_DEV - 1 + TENSOR - 1)

    def v_step(s, _):
        y = product(0, s).astype(BF16)
        send_tile(0, tile_at(s), [y[j * ROWS:(j + 1) * ROWS, hh * 128:(hh + 1) * 128]
                                  for hh in range(2) for j in range(2)])
        return 0

    lax.fori_loop(0, TILES, v_step, 0)

    def kq_step(mat, s, acc):
        y = product(mat, s)
        raw[mat - 1, :, pl.ds(pl.multiple_of(tile_at(s) * WIDE, WIDE), WIDE)] = y
        return acc + (y[:, :128] * y[:, :128] + y[:, 128:] * y[:, 128:])

    rows_i = lax.broadcasted_iota(jnp.int32, (PAIR_ROWS, PAIR_ROWS), 0)
    cols_i = lax.broadcasted_iota(jnp.int32, (PAIR_ROWS, PAIR_ROWS), 1)
    eye = rows_i == cols_i

    def ss_copy(mat, d):
        return pltpu.make_async_remote_copy(
            src_ref=ssend.at[mat - 1], dst_ref=srecv.at[mat - 1, d - 1],
            send_sem=ss_send_sem.at[mat - 1, d - 1], recv_sem=ss_sem.at[mat - 1, d - 1],
            device_id={"tensor": lax.rem(t + d, TENSOR)}, device_id_type=MESH)

    def send_sums(mat, acc):
        col = jnp.sum(acc, axis=1, keepdims=True)
        row = jnp.sum(jnp.where(eye, col, 0.0), axis=0, keepdims=True)
        ssend[mat - 1] = jnp.broadcast_to(row, (8, PAIR_ROWS))
        for d in range(1, TENSOR):
            ss_copy(mat, d).start()

    def norm_send(mat, gain_ref):
        total = ssend[mat - 1]
        for d in range(1, TENSOR):
            ss_copy(mat, d).wait_recv()
            total = total + srecv[mat - 1, d - 1]
        col = jnp.sum(jnp.where(eye, total[0:1, :], 0.0), axis=1, keepdims=True)
        scale = lax.rsqrt(col / float(HEADS * HEAD_DIM) + 1e-06)

        def step(s, _):
            tile = tile_at(s)
            cols = pl.ds(pl.multiple_of(tile * WIDE, WIDE), WIDE)
            y = raw[mat - 1, :, cols] * scale * gain_ref[:, cols]
            blocks = []
            for hh in range(2):
                for j in range(2):
                    u = y[j * ROWS:(j + 1) * ROWS, hh * 128:(hh + 1) * 128]
                    turned = u * tabs[0] + pltpu.roll(u, HEAD_DIM // 2, 1) * tabs[1]
                    blocks.append(turned.astype(BF16))
            send_tile(mat, tile, blocks)
            return 0

        lax.fori_loop(0, TILES, step, 0)

    zero = jnp.zeros((PAIR_ROWS, 128), F32)
    acc = lax.fori_loop(0, TILES, lambda s, a: kq_step(1, s, a), zero)
    send_sums(1, acc)
    acc = lax.fori_loop(0, 3, lambda s, a: kq_step(2, s, a), zero)
    norm_send(1, gk_ref)
    acc = lax.fori_loop(3, TILES, lambda s, a: kq_step(2, s, a), acc)
    send_sums(2, acc)
    wo_copy = pltpu.make_async_copy(wo_hbm, wobuf, wosem)
    wo_copy.start()
    norm_send(2, gq_ref)

    my_z = me // 4
    my_x = lax.rem(me, 4)
    shifted = lax.rem(my_z + 8 - 2 * my_x + 8, 8)
    my_tile = (5 * shifted + 4) // 8
    attends = (8 * my_tile) // 5 == shifted
    head = my_tile * 2 + my_x // 2
    j_mine = lax.rem(my_x, 2)

    @pl.when(attends)
    def _():
        for mat in range(3):
            pltpu.make_async_copy(recv.at[mat], recv.at[mat], recv_sem.at[mat]).wait()
        scale = float(HEAD_DIM ** -0.5 * np.log2(np.e))
        diag = (lax.broadcasted_iota(jnp.int32, (QB, QB), 0) >= lax.broadcasted_iota(jnp.int32, (QB, QB), 1))
        for b in range(SEQ_DEV * ROWS // QB):
            q = recv[2, b * QB:(b + 1) * QB, :]
            last = lax.dot_general(q, recv[1, b * QB:(b + 1) * QB, :], (((1,), (1,)), ((), ())),
                                   preferred_element_type=F32)
            last = jnp.where(diag, last, -1e30)
            top = jnp.max(last, axis=1, keepdims=True)
            if b > 0:
                past = lax.dot_general(q, recv[1, 0:b * QB, :], (((1,), (1,)), ((), ())),
                                       preferred_element_type=F32)
                top = jnp.maximum(top, jnp.max(past, axis=1, keepdims=True))
                e_past = jnp.exp2((past - top) * scale)
            e_last = jnp.exp2((last - top) * scale)
            total = jnp.sum(e_last, axis=1, keepdims=True)
            o = jnp.dot(e_last.astype(BF16), recv[0, b * QB:(b + 1) * QB, :], preferred_element_type=F32)
            if b > 0:
                total = total + jnp.sum(e_past, axis=1, keepdims=True)
                o = o + jnp.dot(e_past.astype(BF16), recv[0, 0:b * QB, :], preferred_element_type=F32)
            amix[b * QB:(b + 1) * QB, :] = (o / total).astype(BF16)
            for k in range(QB // ROWS):
                dest = b * (QB // ROWS) + k
                src = amix.at[pl.ds(dest * ROWS, ROWS), :]
                dst = mixed.at[pl.ds(pl.multiple_of(j_mine * ROWS, ROWS), ROWS),
                               pl.ds(pl.multiple_of(head * 128, 128), 128)]

                @pl.when(dest != me)
                def _():
                    pltpu.make_async_remote_copy(
                        src_ref=src, dst_ref=dst, send_sem=mix_send_sem, recv_sem=mix_sem,
                        device_id={"seq": jnp.int32(dest)}, device_id_type=MESH).start()

                @pl.when(dest == me)
                def _():
                    pltpu.make_async_copy(src, dst, mix_sem).start()

    wo_copy.wait()
    pltpu.make_async_copy(mixed, mixed, mix_sem).wait()
    swap = (cols_i == lax.rem(rows_i, 2) * ROWS + rows_i // 2).astype(F32).astype(BF16)
    perm[...] = jnp.dot(swap, mixed[...], preferred_element_type=F32).astype(BF16)
    out_rows = PAIR_ROWS // TENSOR

    def o_step(c, _):
        cols = pl.ds(pl.multiple_of(c * CHUNK, CHUNK), CHUNK)
        y = jnp.dot(perm[...], wobuf[:, cols], preferred_element_type=F32)
        part[...] = y
        osend[:, cols] = y.astype(BF16)
        oself[:, cols] = part[pl.ds(pl.multiple_of(t * out_rows, out_rows), out_rows), :]
        for d in range(1, TENSOR):
            peer = lax.rem(t + d, TENSOR)
            pltpu.make_async_remote_copy(
                src_ref=osend.at[pl.ds(pl.multiple_of(peer * out_rows, out_rows), out_rows), cols],
                dst_ref=orecv.at[d - 1, :, cols],
                send_sem=o_send_sem.at[d - 1], recv_sem=o_sem.at[d - 1],
                device_id={"tensor": peer}, device_id_type=MESH).start()
        return 0

    lax.fori_loop(0, D // CHUNK, o_step, 0)
    for d in range(1, TENSOR):
        pltpu.make_async_copy(orecv.at[d - 1], orecv.at[d - 1], o_sem.at[d - 1]).wait()

    def sum_step(c, _):
        cols = pl.ds(pl.multiple_of(c * CHUNK, CHUNK), CHUNK)
        y = oself[:, cols]
        for d in range(1, TENSOR):
            y = y + orecv[d - 1, :, cols].astype(F32)
        out_ref[:, cols] = y.astype(BF16)
        return 0

    lax.fori_loop(0, D // CHUNK, sum_step, 0)

    for mat in range(1, 3):
        for d in range(1, TENSOR):
            ss_copy(mat, d).wait_send()
    for d in range(1, TENSOR):
        pltpu.make_async_copy(orecv.at[d - 1], orecv.at[d - 1], o_send_sem.at[d - 1]).wait()

    @pl.when(attends)
    def _():
        for mat in range(3):
            left = send.at[mat, pl.ds(0, 4 * TILES - 1)]
            pltpu.make_async_copy(left, left, send_sem.at[mat]).wait()
        left = amix.at[pl.ds(0, (SEQ_DEV - 1) * ROWS), :]
        pltpu.make_async_copy(left, left, mix_send_sem).wait()

    @pl.when(jnp.logical_not(attends))
    def _():
        for mat in range(3):
            pltpu.make_async_copy(send.at[mat], send.at[mat], send_sem.at[mat]).wait()


def local(tokens, w_query, w_key, w_value, w_out, gain_query, gain_key):
    flat = jnp.transpose(tokens, (1, 0, 2)).reshape(PAIR_ROWS, D)
    half = HEAD_DIM // 2
    freqs = jnp.exp(-jnp.log(500000.0) * jnp.arange(half, dtype=F32) * 2.0 / HEAD_DIM)
    freq_row = jnp.concatenate([freqs, freqs])[None, :]
    dma = pltpu.SemaphoreType.DMA
    vmem = pl.BlockSpec(memory_space=pltpu.VMEM)
    hbm = pl.BlockSpec(memory_space=pl.ANY)
    out_rows = PAIR_ROWS // TENSOR
    out = pl.pallas_call(
        kernel,
        out_shape=jax.ShapeDtypeStruct((out_rows, D), BF16),
        in_specs=[vmem] * 4 + [hbm] * 4,
        out_specs=vmem,
        scratch_shapes=[
            pltpu.VMEM((SLOTS, D, WIDE), BF16),
            pltpu.VMEM((LOCAL, D), BF16),
            pltpu.VMEM((2, PAIR_ROWS, LOCAL), F32),
            pltpu.VMEM((3, 4 * TILES, ROWS, 128), BF16),
            pltpu.VMEM((3, SEQ_DEV * ROWS, 128), BF16),
            pltpu.VMEM((SEQ_DEV * ROWS, 128), BF16),
            pltpu.VMEM((PAIR_ROWS, LOCAL), BF16),
            pltpu.VMEM((PAIR_ROWS, LOCAL), BF16),
            pltpu.VMEM((PAIR_ROWS, CHUNK), F32),
            pltpu.VMEM((PAIR_ROWS, D), BF16),
            pltpu.VMEM((TENSOR - 1, out_rows, D), BF16),
            pltpu.VMEM((out_rows, D), F32),
            pltpu.VMEM((2, 8, PAIR_ROWS), F32),
            pltpu.VMEM((2, TENSOR - 1, 8, PAIR_ROWS), F32),
            pltpu.VMEM((2, ROWS, HEAD_DIM), F32),
            dma((SLOTS,)), dma, dma((3,)), dma((3,)), dma, dma,
            dma((2, TENSOR - 1)), dma((2, TENSOR - 1)), dma((TENSOR - 1,)), dma((TENSOR - 1,)),
        ],
        compiler_params=pltpu.CompilerParams(
            collective_id=0, has_side_effects=True, vmem_limit_bytes=60 * 1024 * 1024),
        name="layer",
    )(flat, gain_query[None, :], gain_key[None, :], freq_row, w_query, w_key, w_value, w_out)
    return out.reshape(out_rows // 2, 2, D)


def solution(mesh):
    return jax.shard_map(
        local,
        mesh=mesh,
        in_specs=(
            P("seq", "dp", None),
            P(None, "tensor"),
            P(None, "tensor"),
            P(None, "tensor"),
            P("tensor", None),
            P("tensor"),
            P("tensor"),
        ),
        out_specs=P(("seq", "tensor"), "dp", None),
        check_vma=False,
    )
```

time: 316 us -> 76.3 us (0.24)
  the two profiles are of different devices: /device:TPU:192 before, /device:TPU:230 now
where the time goes in v1:
time: 76.3 us; the launch traced here: 76 us
  Pallas kernels  68.3 us (90%)
  local copies, waits for them, and re-layouts  7.03 us (9%)
    pallas_call x1, Pallas kernels, local(): pl.pallas_call(kernel, out_shape=jax.ShapeDtypeStruct((out_rows, D), BF16...  68.3 us
    transpose x1, local copies, waits for them, and re-layouts, local(): flat = jnp.transpose(tokens, (1, 0, 2)).reshape(PAIR_ROWS, D)  2.63 us
    reshape x1, local copies, waits for them, and re-layouts, local(): return out.reshape(out_rows // 2, 2, D)  1.82 us

profile of v1, /device:TPU:230, one launch (start us, length us, event | category | flops | bytes accessed | tf_op | source)
XLA Modules:
  0.0 76.0 jit_solution(8344622379423908634)
XLA Ops:
  0.0 0.7 maximum_bitcast_fusion.freq_ref
  0.7 1.3 %broadcast_in_dim.9.gq_ref = f32[1,1280]{1,0:T(1,128)} reshape(f32[1280]{0:T(1024)} %param.12) | data formatting | bytes 10240 | tf_op jit(solution)/shard_map/broadcast_in_dim | solution.py:312
  2.0 1.3 %broadcast_in_dim.10.gk_ref = f32[1,1280]{1,0:T(1,128)} reshape(f32[1280]{0:T(1024)} %param.13) | data formatting | bytes 10240 | tf_op jit(solution)/shard_map/broadcast_in_dim | solution.py:312
  3.3 2.6 %copy.8 = bf16[2,64,5120]{2,1,0:T(8,128)(2,1)} copy(bf16[2,64,5120]{2,0,1:T(2,128)(2,1)} %bitcast.5) | data formatting | bytes 2621440 | tf_op jit(solution)/shard_map/transpose | solution.py:277
  5.9 68.3 %layer.1 = bf16[32,5120]{1,0:T(8,128)(2,1)} custom-call(bf16[128,5120]{1,0:T(8,128)(2,1)} %bitcast.4, f32[1,1280]{1,0:T(1,128)} %broadcast_in_dim.9.gq_ref, f32[1,1280]{1,0:T(1,128)} %broadcast_in_dim.10.gk_ref, f32[1,128]{1,0:T(1,128)} %maximum_bitcast_fusion.freq_ref, bf16[5120,1280]{1,0:T(8,128)(2,1)} %wq_hbm.1, bf16[5120,1280]{1,0:T(8,128)(2,1)} %wk_hbm.1, ...), custom_call_target="tpu_custom_call" | custom-call | tf_op jit(solution)/shard_map/layer/pallas_call | solution.py:285
  74.2 1.8 %reshape.7 = bf16[16,2,5120]{2,1,0:T(2,128)(2,1)} reshape(bf16[32,5120]{1,0:T(8,128)(2,1)} %layer.1) | data formatting | bytes 655360 | tf_op jit(solution)/shard_map/reshape | solution.py:313
  (1 shorter events, 0.0 us)

commit v2 on v1

--- a/solution.py
+++ b/solution.py
@@ -32,9 +32,9 @@
     return z * 4 + x
 
 
-def kernel(x_ref, gq_ref, gk_ref, freq_ref, wq_hbm, wk_hbm, wv_hbm, wo_hbm, out_ref,
-           wbuf, wobuf, raw, send, recv, amix, mixed, perm, part, osend, orecv, oself,
-           ssend, srecv, tabs, wsem, wosem, send_sem, recv_sem, mix_send_sem, mix_sem,
+def kernel(tok_hbm, gq_ref, gk_ref, freq_ref, wq_hbm, wk_hbm, wv_hbm, wo_hbm, out_ref,
+           tok, x_ref, wbuf, wobuf, raw, send, recv, amix, mixed, perm, part, osend, orecv, oself,
+           ssend, srecv, tabs, tok_sem, wsem, wosem, send_sem, recv_sem, mix_send_sem, mix_sem,
            ss_send_sem, ss_sem, o_send_sem, o_sem):
     me = lax.axis_index("seq")
     t = lax.axis_index("tensor")
@@ -58,6 +58,8 @@
         cols = pl.ds(pl.multiple_of(tile_at(s) * WIDE, WIDE), WIDE)
         return pltpu.make_async_copy(weights[mat].at[:, cols], wbuf.at[slot], wsem.at[slot])
 
+    tok_copy = pltpu.make_async_copy(tok_hbm, tok, tok_sem)
+    tok_copy.start()
     for s in range(AHEAD):
         w_copy(0, s).start()
 
@@ -104,6 +106,18 @@
     tabs[0] = jnp.cos(angle)
     tabs[1] = jnp.where(lane < HEAD_DIM // 2, -sine, sine)
 
+    rows_i = lax.broadcasted_iota(jnp.int32, (PAIR_ROWS, PAIR_ROWS), 0)
+    cols_i = lax.broadcasted_iota(jnp.int32, (PAIR_ROWS, PAIR_ROWS), 1)
+    apart = (cols_i == 2 * lax.rem(rows_i, ROWS) + rows_i // ROWS).astype(F32).astype(BF16)
+    tok_copy.wait()
+
+    def x_step(c, _):
+        cols = pl.ds(pl.multiple_of(c * CHUNK, CHUNK), CHUNK)
+        y = tok[:, :, cols].reshape(PAIR_ROWS, CHUNK)
+        x_ref[:, cols] = jnp.dot(apart, y, preferred_element_type=F32).astype(BF16)
+        return 0
+
+    lax.fori_loop(0, D // CHUNK, x_step, 0)
     pl.semaphore_wait(barrier, SEQ_DEV - 1 + TENSOR - 1)
 
     def v_step(s, _):
@@ -119,8 +133,6 @@
         raw[mat - 1, :, pl.ds(pl.multiple_of(tile_at(s) * WIDE, WIDE), WIDE)] = y
         return acc + (y[:, :128] * y[:, :128] + y[:, 128:] * y[:, 128:])
 
-    rows_i = lax.broadcasted_iota(jnp.int32, (PAIR_ROWS, PAIR_ROWS), 0)
-    cols_i = lax.broadcasted_iota(jnp.int32, (PAIR_ROWS, PAIR_ROWS), 1)
     eye = rows_i == cols_i
 
     def ss_copy(mat, d):
@@ -147,7 +159,7 @@
         def step(s, _):
             tile = tile_at(s)
             cols = pl.ds(pl.multiple_of(tile * WIDE, WIDE), WIDE)
-            y = raw[mat - 1, :, cols] * scale * gain_ref[:, cols]
+            y = raw[mat - 1, :, cols] * scale * gain_ref[cols][None, :]
             blocks = []
             for hh in range(2):
                 for j in range(2):
@@ -248,7 +260,7 @@
         y = oself[:, cols]
         for d in range(1, TENSOR):
             y = y + orecv[d - 1, :, cols].astype(F32)
-        out_ref[:, cols] = y.astype(BF16)
+        out_ref[:, :, cols] = y.astype(BF16).reshape(out_rows // 2, 2, CHUNK)
         return 0
 
     lax.fori_loop(0, D // CHUNK, sum_step, 0)
@@ -274,20 +286,21 @@
 
 
 def local(tokens, w_query, w_key, w_value, w_out, gain_query, gain_key):
-    flat = jnp.transpose(tokens, (1, 0, 2)).reshape(PAIR_ROWS, D)
-    half = HEAD_DIM // 2
-    freqs = jnp.exp(-jnp.log(500000.0) * jnp.arange(half, dtype=F32) * 2.0 / HEAD_DIM)
-    freq_row = jnp.concatenate([freqs, freqs])[None, :]
+    idx = np.arange(HEAD_DIM, dtype=np.float32) % (HEAD_DIM // 2)
+    freqs = np.exp(-np.log(np.float32(500000.0)) * idx * np.float32(2.0) / np.float32(HEAD_DIM))
+    freq_row = jnp.asarray(freqs.astype(np.float32)[None, :])
     dma = pltpu.SemaphoreType.DMA
     vmem = pl.BlockSpec(memory_space=pltpu.VMEM)
     hbm = pl.BlockSpec(memory_space=pl.ANY)
     out_rows = PAIR_ROWS // TENSOR
     out = pl.pallas_call(
         kernel,
-        out_shape=jax.ShapeDtypeStruct((out_rows, D), BF16),
-        in_specs=[vmem] * 4 + [hbm] * 4,
+        out_shape=jax.ShapeDtypeStruct((out_rows // 2, 2, D), BF16),
+        in_specs=[hbm] + [vmem] * 3 + [hbm] * 4,
         out_specs=vmem,
         scratch_shapes=[
+            pltpu.VMEM((ROWS, 2, D), BF16),
+            pltpu.VMEM((PAIR_ROWS, D), BF16),
             pltpu.VMEM((SLOTS, D, WIDE), BF16),
             pltpu.VMEM((LOCAL, D), BF16),
             pltpu.VMEM((2, PAIR_ROWS, LOCAL), F32),
@@ -303,14 +316,14 @@
             pltpu.VMEM((2, 8, PAIR_ROWS), F32),
             pltpu.VMEM((2, TENSOR - 1, 8, PAIR_ROWS), F32),
             pltpu.VMEM((2, ROWS, HEAD_DIM), F32),
-            dma((SLOTS,)), dma, dma((3,)), dma((3,)), dma, dma,
+            dma, dma((SLOTS,)), dma, dma((3,)), dma((3,)), dma, dma,
             dma((2, TENSOR - 1)), dma((2, TENSOR - 1)), dma((TENSOR - 1,)), dma((TENSOR - 1,)),
         ],
         compiler_params=pltpu.CompilerParams(
             collective_id=0, has_side_effects=True, vmem_limit_bytes=60 * 1024 * 1024),
         name="layer",
-    )(flat, gain_query[None, :], gain_key[None, :], freq_row, w_query, w_key, w_value, w_out)
-    return out.reshape(out_rows // 2, 2, D)
+    )(tokens, gain_query, gain_key, freq_row, w_query, w_key, w_value, w_out)
+    return out
 
 
 def solution(mesh):

time: 76.3 us -> 70.3 us (0.921)
  the two profiles are of different devices: /device:TPU:230 before, /device:TPU:192 now
where the time goes in v2:
time: 70.3 us; the launch traced here: 69 us
  Pallas kernels  67.1 us (95%)
  local copies, waits for them, and re-layouts  1.92 us (3%)
    pallas_call x1, Pallas kernels, local(): pl.pallas_call(kernel, out_shape=jax.ShapeDtypeStruct((out_rows // 2, 2,...  67.1 us
    unnamed x1, local copies, waits for them, and re-layouts  1.92 us

profile of v2, /device:TPU:192, one launch (start us, length us, event | category | flops | bytes accessed | tf_op | source)
XLA Modules:
  0.0 69.0 jit_solution(12635513392819470558)
XLA Ops:
  0.0 67.1 %layer.1 = bf16[16,2,5120]{2,1,0:T(2,128)(2,1)} custom-call(bf16[64,2,5120]{2,1,0:T(2,128)(2,1)} %tok_hbm.1, f32[1280]{0:T(1024)} %gq_ref.1, f32[1280]{0:T(1024)} %gk_ref.1, f32[1,128]{1,0:T(1,128)} %constant.2.clone.freq_ref, bf16[5120,1280]{1,0:T(8,128)(2,1)} %wq_hbm.1, bf16[5120,1280]{1,0:T(8,128)(2,1)} %wk_hbm.1, bf16[5120,1280]{1,0:T(8,128)(2,1)} %wv_hbm.1, ...), custom_call_target="tpu_custom_call" | custom-call | tf_op jit(solution)/shard_map/layer/pallas_call | solution.py:296
  67.1 1.9 %copy.10 = bf16[16,2,5120]{2,1,0:T(2,128)(2,1)} copy(bf16[16,2,5120]{2,1,0:T(2,128)(2,1)} %layer.1) | data formatting | bytes 655360

commit v3 on v2

v3 whole, which is shorter than its diff:
```python
import functools

import jax
import jax.numpy as jnp
import numpy as np
from jax import lax
from jax.experimental import pallas as pl
from jax.experimental.pallas import tpu as pltpu
from jax.sharding import PartitionSpec as P

HEADS = 40
HEAD_DIM = 128
D = 5120
SEQ_DEV = 32
TENSOR = 4
ROWS = 64
PAIR_ROWS = 128
LOCAL = 1280
TILES = 5
WIDE = 256
SLOTS = 4
AHEAD = 3
CHUNK = 1280
QB = 256
OWNERS = QB // ROWS
GROUPS = 2
MESH = pl.DeviceIdType.MESH
F32 = jnp.float32
BF16 = jnp.bfloat16


def pair_device(head, j, core):
    x = lax.rem(head + 2 * j, 4)
    z = lax.rem(3 * (head // 4) + lax.rem(head, 4) // 2 + 2 * x + 4 * core, 8)
    return z * 4 + x


def kernel(tok_hbm, gq_hbm, gk_hbm, freq_hbm, wq_hbm, wk_hbm, wv_hbm, wo_hbm, out_ref,
           tok, x_ref, gq_ref, gk_ref, freq_ref, wbuf, wobuf, raw, send, recv, amix, mixed, part, osend, orecv, oself,
           ssend, srecv, tabs, tok_sem, gain_sem, wsem, wosem, send_sem, recv_sem, mix_send_sem, mix_sem,
           ss_send_sem, ss_sem, o_send_sem, o_sem):
    me = lax.axis_index("seq")
    t = lax.axis_index("tensor")
    core = lax.axis_index("dp")
    barrier = pltpu.get_barrier_semaphore()

    weights = (wv_hbm, wk_hbm, wq_hbm)

    def tile_at(s):
        return lax.rem(s + me, TILES)

    def w_copy(mat, s):
        slot = lax.rem(mat * TILES + s, SLOTS)
        cols = pl.ds(pl.multiple_of(tile_at(s) * WIDE, WIDE), WIDE)
        return pltpu.make_async_copy(weights[mat].at[:, cols], wbuf.at[slot], wsem.at[slot])


    tok_copy = pltpu.make_async_copy(tok_hbm, tok, tok_sem)
    tok_copy.start()
    for s in range(AHEAD):
        w_copy(0, s).start()

    small = [pltpu.make_async_copy(a, b, gain_sem.at[k]) for k, (a, b) in
             enumerate(((gq_hbm, gq_ref), (gk_hbm, gk_ref), (freq_hbm, freq_ref)))]
    for copy in small:
        copy.start()

    def greet(d, _):
        pl.semaphore_signal(barrier, inc=1, device_id={"seq": lax.rem(me + d, SEQ_DEV)}, device_id_type=MESH)
        return 0

    lax.fori_loop(1, SEQ_DEV, greet, 0)
    for d in range(1, TENSOR):
        pl.semaphore_signal(barrier, inc=1, device_id={"tensor": lax.rem(t + d, TENSOR)}, device_id_type=MESH)

    def prefetch(mat, s):
        later = s + AHEAD

        @pl.when(later < TILES)
        def _():
            w_copy(mat, later).start()

        if mat < 2:
            @pl.when(later >= TILES)
            def _():
                w_copy(mat + 1, later - TILES).start()

    def product(mat, s):
        prefetch(mat, s)
        w_copy(mat, s).wait()
        slot = lax.rem(mat * TILES + s, SLOTS)
        return jnp.dot(x_ref[...], wbuf[slot], preferred_element_type=F32)

    def start_pair(mat, head, j):
        dest = pair_device(head, j, core)
        src = send.at[mat, head * 2 + j]
        dst = recv.at[mat, me]

        @pl.when(dest != me)
        def _():
            pltpu.make_async_remote_copy(
                src_ref=src, dst_ref=dst, send_sem=send_sem.at[mat], recv_sem=recv_sem.at[mat],
                device_id={"seq": dest}, device_id_type=MESH).start()

        @pl.when(dest == me)
        def _():
            pltpu.make_async_copy(src, dst, recv_sem.at[mat]).start()

    def send_tile(mat, tile, y, sequences):
        y = jnp.dot(apart, y, preferred_element_type=F32).astype(BF16)
        for hh in range(2):
            for j in range(2):
                send[mat, tile * 4 + hh * 2 + j] = y[j * ROWS:(j + 1) * ROWS, hh * 128:(hh + 1) * 128]
        for hh in range(2):
            for j in sequences:
                start_pair(mat, tile * 2 + hh, j)

    rows_i = lax.broadcasted_iota(jnp.int32, (PAIR_ROWS, PAIR_ROWS), 0)
    cols_i = lax.broadcasted_iota(jnp.int32, (PAIR_ROWS, PAIR_ROWS), 1)
    apart = (cols_i == 2 * lax.rem(rows_i, ROWS) + rows_i // ROWS).astype(F32).astype(BF16)
    tok_copy.wait()

    def x_step(c, _):
        cols = pl.ds(pl.multiple_of(c * CHUNK, CHUNK), CHUNK)
        x_ref[:, cols] = tok[:, :, cols].reshape(PAIR_ROWS, CHUNK)
        return 0

    lax.fori_loop(0, D // CHUNK, x_step, 0)

    first = product(0, 0).astype(BF16)
    pl.semaphore_wait(barrier, SEQ_DEV - 1 + TENSOR - 1)
    send_tile(0, tile_at(0), first, (0, 1))

    def v_step(s, _):
        send_tile(0, tile_at(s), product(0, s).astype(BF16), (0, 1))
        return 0

    lax.fori_loop(1, TILES, v_step, 0)

    for copy in small:
        copy.wait()
    lane = lax.broadcasted_iota(jnp.int32, (PAIR_ROWS, HEAD_DIM), 1)
    pos = lax.broadcasted_iota(jnp.int32, (PAIR_ROWS, HEAD_DIM), 0) // 2 + me * ROWS
    angle = pos.astype(F32) * freq_ref[...]
    sine = jnp.sin(angle)
    tabs[0] = jnp.cos(angle)
    tabs[1] = jnp.where(lane < HEAD_DIM // 2, -sine, sine)

    def kq_step(mat, s, acc):
        y = product(mat, s)
        raw[mat - 1, :, pl.ds(pl.multiple_of(tile_at(s) * WIDE, WIDE), WIDE)] = y
        return acc + (y[:, :128] * y[:, :128] + y[:, 128:] * y[:, 128:])

    eye = rows_i == cols_i

    def ss_copy(mat, d):
        return pltpu.make_async_remote_copy(
            src_ref=ssend.at[mat - 1], dst_ref=srecv.at[mat - 1, d - 1],
            send_sem=ss_send_sem.at[mat - 1, d - 1], recv_sem=ss_sem.at[mat - 1, d - 1],
            device_id={"tensor": lax.rem(t + d, TENSOR)}, device_id_type=MESH)

    def send_sums(mat, acc):
        col = jnp.sum(acc, axis=1, keepdims=True)
        row = jnp.sum(jnp.where(eye, col, 0.0), axis=0, keepdims=True)
        ssend[mat - 1] = jnp.broadcast_to(row, (8, PAIR_ROWS))
        for d in range(1, TENSOR):
            ss_copy(mat, d).start()

    def norm_send(mat, gain_ref):
        total = ssend[mat - 1]
        for d in range(1, TENSOR):
            ss_copy(mat, d).wait_recv()
            total = total + srecv[mat - 1, d - 1]
        col = jnp.sum(jnp.where(eye, total[0:1, :], 0.0), axis=1, keepdims=True)
        scale = lax.rsqrt(col / float(HEADS * HEAD_DIM) + 1e-06)

        def step(s, _):
            tile = tile_at(s)
            cols = pl.ds(pl.multiple_of(tile * WIDE, WIDE), WIDE)
            y = raw[mat - 1, :, cols] * scale * gain_ref[cols][None, :]
            turned = []
            for hh in range(2):
                u = y[:, hh * 128:(hh + 1) * 128]
                turned.append((u * tabs[0] + pltpu.roll(u, HEAD_DIM // 2, 1) * tabs[1]).astype(BF16))
            send_tile(mat, tile, jnp.concatenate(turned, axis=1), (0,))
            return 0

        lax.fori_loop(0, TILES, step, 0)

    zero = jnp.zeros((PAIR_ROWS, 128), F32)
    acc = lax.fori_loop(0, TILES, lambda s, a: kq_step(1, s, a), zero)
    send_sums(1, acc)
    acc = lax.fori_loop(0, 3, lambda s, a: kq_step(2, s, a), zero)
    norm_send(1, gk_ref)
    acc = lax.fori_loop(3, TILES, lambda s, a: kq_step(2, s, a), acc)
    send_sums(2, acc)
    wo_copy = pltpu.make_async_copy(wo_hbm, wobuf, wosem)
    wo_copy.start()
    norm_send(2, gq_ref)

    def second(k, _):
        head = lax.rem(k + 2 * me, 2 * TILES)
        start_pair(1, head, 1)
        start_pair(2, head, 1)
        return 0

    lax.fori_loop(0, 2 * TILES, second, 0)

    my_z = me // 4
    my_x = lax.rem(me, 4)
    shifted = lax.rem(my_z + 16 - 2 * my_x - 4 * core, 8)
    group = shifted // 3
    side = lax.rem(shifted, 3)
    attends = jnp.logical_and(side < 2, shifted < 7)
    head = jnp.minimum(4 * group + 2 * side + lax.rem(my_x, 2), 2 * TILES - 1)
    j_mine = lax.rem(my_x // 2 + side, 2)

    @pl.when(attends)
    def _():
        for mat in range(3):
            pltpu.make_async_copy(recv.at[mat], recv.at[mat], recv_sem.at[mat]).wait()
        scale = float(HEAD_DIM ** -0.5 * np.log2(np.e))
        causal = (lax.broadcasted_iota(jnp.int32, (QB, QB), 0) >= lax.broadcasted_iota(jnp.int32, (QB, QB), 1))
        dst = mixed.at[j_mine, :, pl.ds(pl.multiple_of(head * 128, 128), 128)]
        group_size = SEQ_DEV // GROUPS
        for g in range(GROUPS):
            for b in range(g * group_size // OWNERS, (g + 1) * group_size // OWNERS):
                own = slice(b * OWNERS, (b + 1) * OWNERS)
                q = recv[2, own].reshape(QB, HEAD_DIM)
                last = lax.dot_general(q, recv[1, own].reshape(QB, HEAD_DIM), (((1,), (1,)), ((), ())),
                                       preferred_element_type=F32)
                last = jnp.where(causal, last, -1e30)
                top = jnp.max(last, axis=1, keepdims=True)
                if b > 0:
                    past = lax.dot_general(q, recv[1, 0:b * OWNERS].reshape(b * QB, HEAD_DIM),
                                           (((1,), (1,)), ((), ())), preferred_element_type=F32)
                    top = jnp.maximum(top, jnp.max(past, axis=1, keepdims=True))
                    e_past = jnp.exp2((past - top) * scale)
                e_last = jnp.exp2((last - top) * scale)
                total = jnp.sum(e_last, axis=1, keepdims=True)
                o = jnp.dot(e_last.astype(BF16), recv[0, own].reshape(QB, HEAD_DIM), preferred_element_type=F32)
                if b > 0:
                    total = total + jnp.sum(e_past, axis=1, keepdims=True)
                    o = o + jnp.dot(e_past.astype(BF16), recv[0, 0:b * OWNERS].reshape(b * QB, HEAD_DIM),
                                    preferred_element_type=F32)
                amix[own] = (o / total).astype(BF16).reshape(OWNERS, ROWS, HEAD_DIM)

            def give(k, _):
                dest = g * group_size + lax.rem(me + k, group_size)

                @pl.when(dest != me)
                def _():
                    pltpu.make_async_remote_copy(
                        src_ref=amix.at[dest], dst_ref=dst, send_sem=mix_send_sem, recv_sem=mix_sem.at[j_mine],
                        device_id={"seq": dest}, device_id_type=MESH).start()

                @pl.when(dest == me)
                def _():
                    pltpu.make_async_copy(amix.at[dest], dst, mix_sem.at[j_mine]).start()
                return 0

            lax.fori_loop(0, group_size, give, 0)

    wo_copy.wait()
    out_rows = ROWS // TENSOR
    for j in range(2):
        pltpu.make_async_copy(mixed.at[j], mixed.at[j], mix_sem.at[j]).wait()

        def o_step(c, _):
            cols = pl.ds(pl.multiple_of(c * CHUNK, CHUNK), CHUNK)
            y = jnp.dot(mixed[j], wobuf[:, cols], preferred_element_type=F32)
            part[...] = y
            osend[j, :, cols] = y.astype(BF16)

            def rows_of(index):
                return pl.ds(pl.multiple_of(index * out_rows, out_rows), out_rows)

            oself[j, :, cols] = part[rows_of(t), :]
            for d in range(1, TENSOR):
                peer = lax.rem(t + d, TENSOR)
                pltpu.make_async_remote_copy(
                    src_ref=osend.at[j, rows_of(peer), cols], dst_ref=orecv.at[j, d - 1, :, cols],
                    send_sem=o_send_sem.at[j, d - 1], recv_sem=o_sem.at[j, d - 1],
                    device_id={"tensor": peer}, device_id_type=MESH).start()
            return 0

        lax.fori_loop(0, D // CHUNK, o_step, 0)

    for j in range(2):
        for d in range(1, TENSOR):
            pltpu.make_async_copy(orecv.at[j, d - 1], orecv.at[j, d - 1], o_sem.at[j, d - 1]).wait()
    rows_o = lax.broadcasted_iota(jnp.int32, (2 * out_rows, 2 * out_rows), 0)
    cols_o = lax.broadcasted_iota(jnp.int32, (2 * out_rows, 2 * out_rows), 1)
    swap = (cols_o == lax.rem(rows_o, 2) * out_rows + rows_o // 2).astype(F32).astype(BF16)

    def sum_step(c, _):
        cols = pl.ds(pl.multiple_of(c * CHUNK, CHUNK), CHUNK)
        both = []
        for j in range(2):
            y = oself[j, :, cols]
            for d in range(1, TENSOR):
                y = y + orecv[j, d - 1, :, cols].astype(F32)
            both.append(y.astype(BF16))
        y = jnp.dot(swap, jnp.concatenate(both, axis=0), preferred_element_type=F32)
        out_ref[:, :, cols] = y.astype(BF16).reshape(out_rows, 2, CHUNK)
        return 0

    lax.fori_loop(0, D // CHUNK, sum_step, 0)

    for mat in range(1, 3):
        for d in range(1, TENSOR):
            ss_copy(mat, d).wait_send()
    for j in range(2):
        for d in range(1, TENSOR):
            pltpu.make_async_copy(orecv.at[j, d - 1], orecv.at[j, d - 1], o_send_sem.at[j, d - 1]).wait()

    @pl.when(attends)
    def _():
        for mat in range(3):
            left = send.at[mat, pl.ds(0, 4 * TILES - 1)]
            pltpu.make_async_copy(left, left, send_sem.at[mat]).wait()
        left = amix.at[pl.ds(0, SEQ_DEV - 1)]
        pltpu.make_async_copy(left, left, mix_send_sem).wait()

    @pl.when(jnp.logical_not(attends))
    def _():
        for mat in range(3):
            pltpu.make_async_copy(send.at[mat], send.at[mat], send_sem.at[mat]).wait()


def local(tokens, w_query, w_key, w_value, w_out, gain_query, gain_key):
    idx = np.arange(HEAD_DIM, dtype=np.float32) % (HEAD_DIM // 2)
    freqs = np.exp(-np.log(np.float32(500000.0)) * idx * np.float32(2.0) / np.float32(HEAD_DIM))
    freq_row = jnp.asarray(freqs.astype(np.float32)[None, :])
    dma = pltpu.SemaphoreType.DMA
    vmem = pl.BlockSpec(memory_space=pltpu.VMEM)
    hbm = pl.BlockSpec(memory_space=pl.ANY)
    out_rows = ROWS // TENSOR
    out = pl.pallas_call(
        kernel,
        out_shape=jax.ShapeDtypeStruct((ROWS // TENSOR, 2, D), BF16),
        in_specs=[hbm] * 8,
        out_specs=vmem,
        scratch_shapes=[
            pltpu.VMEM((ROWS, 2, D), BF16),
            pltpu.VMEM((PAIR_ROWS, D), BF16),
            pltpu.VMEM((LOCAL,), F32),
            pltpu.VMEM((LOCAL,), F32),
            pltpu.VMEM((1, HEAD_DIM), F32),
            pltpu.VMEM((SLOTS, D, WIDE), BF16),
            pltpu.VMEM((LOCAL, D), BF16),
            pltpu.VMEM((2, PAIR_ROWS, LOCAL), F32),
            pltpu.VMEM((3, 4 * TILES, ROWS, 128), BF16),
            pltpu.VMEM((3, SEQ_DEV, ROWS, 128), BF16),
            pltpu.VMEM((SEQ_DEV, ROWS, 128), BF16),
            pltpu.VMEM((2, ROWS, LOCAL), BF16),
            pltpu.VMEM((ROWS, CHUNK), F32),
            pltpu.VMEM((2, ROWS, D), BF16),
            pltpu.VMEM((2, TENSOR - 1, out_rows, D), BF16),
            pltpu.VMEM((2, out_rows, D), F32),
            pltpu.VMEM((2, 8, PAIR_ROWS), F32),
            pltpu.VMEM((2, TENSOR - 1, 8, PAIR_ROWS), F32),
            pltpu.VMEM((2, PAIR_ROWS, HEAD_DIM), F32),
            dma, dma((3,)), dma((SLOTS,)), dma, dma((3,)), dma((3,)), dma, dma((2,)),
            dma((2, TENSOR - 1)), dma((2, TENSOR - 1)), dma((2, TENSOR - 1)), dma((2, TENSOR - 1)),
        ],
        compiler_params=pltpu.CompilerParams(
            collective_id=0, has_side_effects=True, vmem_limit_bytes=60 * 1024 * 1024),
        name="layer",
    )(tokens, gain_query, gain_key, freq_row, w_query, w_key, w_value, w_out)
    return out


def solution(mesh):
    return jax.shard_map(
        local,
        mesh=mesh,
        in_specs=(
            P("seq", "dp", None),
            P(None, "tensor"),
            P(None, "tensor"),
            P(None, "tensor"),
            P("tensor", None),
            P("tensor"),
            P("tensor"),
        ),
        out_specs=P(("seq", "tensor"), "dp", None),
        check_vma=False,
    )
```

time: 70.3 us -> 68 us (0.967); the launches traced: 69 us -> 67.8 us
  Pallas kernels: 67.1 us -> 65.9 us
    pallas_call x1, Pallas kernels: 67.1 us -> 65.9 us  [local(): pl.pallas_call(kernel, out_shape=jax.ShapeDtypeStruct((ROWS // TENSOR, 2,...]
where the time goes in v3:
time: 68 us; the launch traced here: 67.8 us
  Pallas kernels  65.9 us (97%)
  local copies, waits for them, and re-layouts  1.92 us (3%)
    pallas_call x1, Pallas kernels, local(): pl.pallas_call(kernel, out_shape=jax.ShapeDtypeStruct((ROWS // TENSOR, 2,...  65.9 us
    unnamed x1, local copies, waits for them, and re-layouts  1.92 us

profile of v3, /device:TPU:192, one launch (start us, length us, event | category | flops | bytes accessed | tf_op | source)
XLA Modules:
  0.0 67.8 jit_solution(17448166170251636688)
XLA Ops:
  0.0 65.9 %layer.1 = bf16[16,2,5120]{2,1,0:T(2,128)(2,1)} custom-call(bf16[64,2,5120]{2,1,0:T(2,128)(2,1)} %tok_hbm.1, f32[1280]{0:T(1024)} %gq_hbm.1, f32[1280]{0:T(1024)} %gk_hbm.1, f32[1,128]{1,0:T(1,128)} %constant.2.clone.freq_hbm, bf16[5120,1280]{1,0:T(8,128)(2,1)} %wq_hbm.1, bf16[5120,1280]{1,0:T(8,128)(2,1)} %wk_hbm.1, bf16[5120,1280]{1,0:T(8,128)(2,1)} %wv_hbm.1, ...), custom_call_target="tpu_custom_call" | custom-call | tf_op jit(solution)/shard_map/layer/pallas_call | solution.py:339
  65.9 1.9 %copy.10 = bf16[16,2,5120]{2,1,0:T(2,128)(2,1)} copy(bf16[16,2,5120]{2,1,0:T(2,128)(2,1)} %layer.1) | data formatting | bytes 655360

commit v4 on v3

--- a/solution.py
+++ b/solution.py
@@ -23,7 +23,7 @@
 CHUNK = 1280
 QB = 256
 OWNERS = QB // ROWS
-GROUPS = 2
+GROUPS = 4
 MESH = pl.DeviceIdType.MESH
 F32 = jnp.float32
 BF16 = jnp.bfloat16
@@ -56,9 +56,8 @@
 
 
     tok_copy = pltpu.make_async_copy(tok_hbm, tok, tok_sem)
+    w_copy(0, 0).start()
     tok_copy.start()
-    for s in range(AHEAD):
-        w_copy(0, s).start()
 
     small = [pltpu.make_async_copy(a, b, gain_sem.at[k]) for k, (a, b) in
              enumerate(((gq_hbm, gq_ref), (gk_hbm, gk_ref), (freq_hbm, freq_ref)))]
@@ -106,19 +105,33 @@
         def _():
             pltpu.make_async_copy(src, dst, recv_sem.at[mat]).start()
 
-    def send_tile(mat, tile, y, sequences):
+    def keep_tile(mat, tile, y):
         y = jnp.dot(apart, y, preferred_element_type=F32).astype(BF16)
         for hh in range(2):
             for j in range(2):
                 send[mat, tile * 4 + hh * 2 + j] = y[j * ROWS:(j + 1) * ROWS, hh * 128:(hh + 1) * 128]
+
+    def send_tile(mat, tile, y):
+        keep_tile(mat, tile, y)
         for hh in range(2):
-            for j in sequences:
+            for j in range(2):
                 start_pair(mat, tile * 2 + hh, j)
+
+    def send_sequence(mats, j):
+        def step(k, _):
+            head = lax.rem(k + 2 * me, 2 * TILES)
+            for mat in mats:
+                start_pair(mat, head, j)
+            return 0
+
+        lax.fori_loop(0, 2 * TILES, step, 0)
 
     rows_i = lax.broadcasted_iota(jnp.int32, (PAIR_ROWS, PAIR_ROWS), 0)
     cols_i = lax.broadcasted_iota(jnp.int32, (PAIR_ROWS, PAIR_ROWS), 1)
     apart = (cols_i == 2 * lax.rem(rows_i, ROWS) + rows_i // ROWS).astype(F32).astype(BF16)
     tok_copy.wait()
+    for s in range(1, AHEAD):
+        w_copy(0, s).start()
 
     def x_step(c, _):
         cols = pl.ds(pl.multiple_of(c * CHUNK, CHUNK), CHUNK)
@@ -129,10 +142,10 @@
 
     first = product(0, 0).astype(BF16)
     pl.semaphore_wait(barrier, SEQ_DEV - 1 + TENSOR - 1)
-    send_tile(0, tile_at(0), first, (0, 1))
+    send_tile(0, tile_at(0), first)
 
     def v_step(s, _):
-        send_tile(0, tile_at(s), product(0, s).astype(BF16), (0, 1))
+        send_tile(0, tile_at(s), product(0, s).astype(BF16))
         return 0
 
     lax.fori_loop(1, TILES, v_step, 0)
@@ -174,18 +187,15 @@
         col = jnp.sum(jnp.where(eye, total[0:1, :], 0.0), axis=1, keepdims=True)
         scale = lax.rsqrt(col / float(HEADS * HEAD_DIM) + 1e-06)
 
-        def step(s, _):
-            tile = tile_at(s)
-            cols = pl.ds(pl.multiple_of(tile * WIDE, WIDE), WIDE)
+        for tile in range(TILES):
+            cols = pl.ds(tile * WIDE, WIDE)
             y = raw[mat - 1, :, cols] * scale * gain_ref[cols][None, :]
             turned = []
             for hh in range(2):
                 u = y[:, hh * 128:(hh + 1) * 128]
                 turned.append((u * tabs[0] + pltpu.roll(u, HEAD_DIM // 2, 1) * tabs[1]).astype(BF16))
-            send_tile(mat, tile, jnp.concatenate(turned, axis=1), (0,))
-            return 0
-
-        lax.fori_loop(0, TILES, step, 0)
+            keep_tile(mat, tile, jnp.concatenate(turned, axis=1))
+        send_sequence((mat,), 0)
 
     zero = jnp.zeros((PAIR_ROWS, 128), F32)
     acc = lax.fori_loop(0, TILES, lambda s, a: kq_step(1, s, a), zero)
@@ -198,13 +208,7 @@
     wo_copy.start()
     norm_send(2, gq_ref)
 
-    def second(k, _):
-        head = lax.rem(k + 2 * me, 2 * TILES)
-        start_pair(1, head, 1)
-        start_pair(2, head, 1)
-        return 0
-
-    lax.fori_loop(0, 2 * TILES, second, 0)
+    send_sequence((1, 2), 1)
 
     my_z = me // 4
     my_x = lax.rem(me, 4)
@@ -276,7 +280,7 @@
                 return pl.ds(pl.multiple_of(index * out_rows, out_rows), out_rows)
 
             oself[j, :, cols] = part[rows_of(t), :]
-            for d in range(1, TENSOR):
+            for d in (2, 1, 3):
                 peer = lax.rem(t + d, TENSOR)
                 pltpu.make_async_remote_copy(
                     src_ref=osend.at[j, rows_of(peer), cols], dst_ref=orecv.at[j, d - 1, :, cols],
@@ -326,6 +330,10 @@
     def _():
         for mat in range(3):
             pltpu.make_async_copy(send.at[mat], send.at[mat], send_sem.at[mat]).wait()
+
+
+def write_out(y_ref, out_ref):
+    out_ref[...] = y_ref[...]
 
 
 def local(tokens, w_query, w_key, w_value, w_out, gain_query, gain_key):
@@ -368,7 +376,13 @@
             collective_id=0, has_side_effects=True, vmem_limit_bytes=60 * 1024 * 1024),
         name="layer",
     )(tokens, gain_query, gain_key, freq_row, w_query, w_key, w_value, w_out)
-    return out
+    return pl.pallas_call(
+        write_out,
+        out_shape=jax.ShapeDtypeStruct(out.shape, BF16),
+        in_specs=[vmem],
+        out_specs=vmem,
+        name="write_out",
+    )(out)
 
 
 def solution(mesh):

time: 68 us -> 66.9 us (0.984)
  local copies, waits for them, and re-layouts: 1.92 us -> 0 us
  Pallas kernels: 65.9 us -> 66.7 us
    unnamed x1 -> x0, local copies, waits for them, and re-layouts: 1.92 us -> none
    pallas_call x0 -> x1, Pallas kernels: none -> 1.72 us  [local(): pl.pallas_call(write_out, out_shape=jax.ShapeDtypeStruct(out.shape, BF16)...]
    pallas_call x1, Pallas kernels: 65.9 us -> 65 us  [local(): pl.pallas_call(kernel, out_shape=jax.ShapeDtypeStruct((ROWS // TENSOR, 2,...]
where the time goes in v4:
time: 66.9 us; the launch traced here: 66.7 us
  Pallas kernels  66.7 us (100%)
    pallas_call x1, Pallas kernels, local(): pl.pallas_call(kernel, out_shape=jax.ShapeDtypeStruct((ROWS // TENSOR, 2,...  65 us
    pallas_call x1, Pallas kernels, local(): pl.pallas_call(write_out, out_shape=jax.ShapeDtypeStruct(out.shape, BF16)...  1.72 us

profile of v4, /device:TPU:192, one launch (start us, length us, event | category | flops | bytes accessed | tf_op | source)
XLA Modules:
  0.0 66.7 jit_solution(5397846138625832031)
XLA Ops:
  0.0 65.0 %layer.1.y_ref = bf16[16,2,5120]{2,1,0:T(2,128)(2,1)} custom-call(bf16[64,2,5120]{2,1,0:T(2,128)(2,1)} %tok_hbm.1, f32[1280]{0:T(1024)} %gq_hbm.1, f32[1280]{0:T(1024)} %gk_hbm.1, f32[1,128]{1,0:T(1,128)} %constant.2.clone.freq_hbm, bf16[5120,1280]{1,0:T(8,128)(2,1)} %wq_hbm.1, bf16[5120,1280]{1,0:T(8,128)(2,1)} %wk_hbm.1, bf16[5120,1280]{1,0:T(8,128)(2,1)} %wv_hbm.1, ...), custom_call_target="tpu_custom_call" | custom-call | tf_op jit(solution)/shard_map/layer/pallas_call | solution.py:347
  65.0 1.7 %write_out.1 = bf16[16,2,5120]{2,1,0:T(2,128)(2,1)} custom-call(bf16[16,2,5120]{2,1,0:T(2,128)(2,1)} %layer.1.y_ref), custom_call_target="tpu_custom_call" | custom-call | tf_op jit(solution)/shard_map/write_out/pallas_call | solution.py:379

commit v5 on v4

--- a/solution.py
+++ b/solution.py
@@ -22,8 +22,11 @@
 AHEAD = 3
 CHUNK = 1280
 QB = 256
-OWNERS = QB // ROWS
 GROUPS = 4
+PASSES = 2
+PASS_ROWS = ROWS // PASSES
+PASS_TOKENS = ROWS // TENSOR // PASSES
+OWNERS = QB // PASS_ROWS
 MESH = pl.DeviceIdType.MESH
 F32 = jnp.float32
 BF16 = jnp.bfloat16
@@ -33,6 +36,11 @@
     x = lax.rem(head + 2 * j, 4)
     z = lax.rem(3 * (head // 4) + lax.rem(head, 4) // 2 + 2 * x + 4 * core, 8)
     return z * 4 + x
+
+
+def token_of(row):
+    inner = lax.rem(row, PASS_ROWS)
+    return inner // PASS_TOKENS * (ROWS // TENSOR) + row // PASS_ROWS * PASS_TOKENS + lax.rem(inner, PASS_TOKENS)
 
 
 def kernel(tok_hbm, gq_hbm, gk_hbm, freq_hbm, wq_hbm, wk_hbm, wv_hbm, wo_hbm, out_ref,
@@ -128,7 +136,7 @@
 
     rows_i = lax.broadcasted_iota(jnp.int32, (PAIR_ROWS, PAIR_ROWS), 0)
     cols_i = lax.broadcasted_iota(jnp.int32, (PAIR_ROWS, PAIR_ROWS), 1)
-    apart = (cols_i == 2 * lax.rem(rows_i, ROWS) + rows_i // ROWS).astype(F32).astype(BF16)
+    apart = (cols_i == 2 * token_of(lax.rem(rows_i, ROWS)) + rows_i // ROWS).astype(F32).astype(BF16)
     tok_copy.wait()
     for s in range(1, AHEAD):
         w_copy(0, s).start()
@@ -224,68 +232,79 @@
         for mat in range(3):
             pltpu.make_async_copy(recv.at[mat], recv.at[mat], recv_sem.at[mat]).wait()
         scale = float(HEAD_DIM ** -0.5 * np.log2(np.e))
-        causal = (lax.broadcasted_iota(jnp.int32, (QB, QB), 0) >= lax.broadcasted_iota(jnp.int32, (QB, QB), 1))
-        dst = mixed.at[j_mine, :, pl.ds(pl.multiple_of(head * 128, 128), 128)]
+        span = OWNERS * ROWS
+        q_row = lax.broadcasted_iota(jnp.int32, (QB, 1), 0)
+        k_row = lax.broadcasted_iota(jnp.int32, (1, span), 1)
+        k_pos = k_row // ROWS * ROWS + token_of(lax.rem(k_row, ROWS))
+        cols = pl.ds(pl.multiple_of(head * 128, 128), 128)
         group_size = SEQ_DEV // GROUPS
         for g in range(GROUPS):
-            for b in range(g * group_size // OWNERS, (g + 1) * group_size // OWNERS):
-                own = slice(b * OWNERS, (b + 1) * OWNERS)
-                q = recv[2, own].reshape(QB, HEAD_DIM)
-                last = lax.dot_general(q, recv[1, own].reshape(QB, HEAD_DIM), (((1,), (1,)), ((), ())),
-                                       preferred_element_type=F32)
-                last = jnp.where(causal, last, -1e30)
-                top = jnp.max(last, axis=1, keepdims=True)
-                if b > 0:
-                    past = lax.dot_general(q, recv[1, 0:b * OWNERS].reshape(b * QB, HEAD_DIM),
-                                           (((1,), (1,)), ((), ())), preferred_element_type=F32)
-                    top = jnp.maximum(top, jnp.max(past, axis=1, keepdims=True))
-                    e_past = jnp.exp2((past - top) * scale)
-                e_last = jnp.exp2((last - top) * scale)
-                total = jnp.sum(e_last, axis=1, keepdims=True)
-                o = jnp.dot(e_last.astype(BF16), recv[0, own].reshape(QB, HEAD_DIM), preferred_element_type=F32)
-                if b > 0:
-                    total = total + jnp.sum(e_past, axis=1, keepdims=True)
-                    o = o + jnp.dot(e_past.astype(BF16), recv[0, 0:b * OWNERS].reshape(b * QB, HEAD_DIM),
-                                    preferred_element_type=F32)
-                amix[own] = (o / total).astype(BF16).reshape(OWNERS, ROWS, HEAD_DIM)
-
-            def give(k, _):
-                dest = g * group_size + lax.rem(me + k, group_size)
-
-                @pl.when(dest != me)
-                def _():
-                    pltpu.make_async_remote_copy(
-                        src_ref=amix.at[dest], dst_ref=dst, send_sem=mix_send_sem, recv_sem=mix_sem.at[j_mine],
-                        device_id={"seq": dest}, device_id_type=MESH).start()
-
-                @pl.when(dest == me)
-                def _():
-                    pltpu.make_async_copy(amix.at[dest], dst, mix_sem.at[j_mine]).start()
-                return 0
-
-            lax.fori_loop(0, group_size, give, 0)
+            for p in range(PASSES):
+                q_pos = q_row // PASS_ROWS * ROWS + token_of(p * PASS_ROWS + lax.rem(q_row, PASS_ROWS))
+                for b in range(g * group_size // OWNERS, (g + 1) * group_size // OWNERS):
+                    own = slice(b * OWNERS, (b + 1) * OWNERS)
+                    q = recv[2, own, p * PASS_ROWS:(p + 1) * PASS_ROWS, :].reshape(QB, HEAD_DIM)
+                    last = lax.dot_general(q, recv[1, own].reshape(span, HEAD_DIM), (((1,), (1,)), ((), ())),
+                                           preferred_element_type=F32)
+                    last = jnp.where(q_pos >= k_pos, last, -1e30)
+                    top = jnp.max(last, axis=1, keepdims=True)
+                    if b > 0:
+                        past = lax.dot_general(q, recv[1, 0:b * OWNERS].reshape(b * span, HEAD_DIM),
+                                               (((1,), (1,)), ((), ())), preferred_element_type=F32)
+                        top = jnp.maximum(top, jnp.max(past, axis=1, keepdims=True))
+                        e_past = jnp.exp2((past - top) * scale)
+                    e_last = jnp.exp2((last - top) * scale)
+                    total = jnp.sum(e_last, axis=1, keepdims=True)
+                    o = jnp.dot(e_last.astype(BF16), recv[0, own].reshape(span, HEAD_DIM),
+                                preferred_element_type=F32)
+                    if b > 0:
+                        total = total + jnp.sum(e_past, axis=1, keepdims=True)
+                        o = o + jnp.dot(e_past.astype(BF16), recv[0, 0:b * OWNERS].reshape(b * span, HEAD_DIM),
+                                        preferred_element_type=F32)
+                    amix[p, own] = (o / total).astype(BF16).reshape(OWNERS, PASS_ROWS, HEAD_DIM)
+                dst = mixed.at[j_mine, p * PASS_ROWS:(p + 1) * PASS_ROWS, cols]
+
+                def give(k, _):
+                    dest = g * group_size + lax.rem(me + k, group_size)
+
+                    @pl.when(dest != me)
+                    def _():
+                        pltpu.make_async_remote_copy(
+                            src_ref=amix.at[p, dest], dst_ref=dst, send_sem=mix_send_sem.at[p],
+                            recv_sem=mix_sem.at[j_mine, p], device_id={"seq": dest}, device_id_type=MESH).start()
+
+                    @pl.when(dest == me)
+                    def _():
+                        pltpu.make_async_copy(amix.at[p, dest], dst, mix_sem.at[j_mine, p]).start()
+                    return 0
+
+                lax.fori_loop(0, group_size, give, 0)
 
     wo_copy.wait()
     out_rows = ROWS // TENSOR
-    for j in range(2):
-        pltpu.make_async_copy(mixed.at[j], mixed.at[j], mix_sem.at[j]).wait()
+    for j, passes in ((0, (0, 1)), (1, (0,)), (1, (1,))):
+        for p in passes:
+            part_rows = mixed.at[j, p * PASS_ROWS:(p + 1) * PASS_ROWS]
+            pltpu.make_async_copy(part_rows, part_rows, mix_sem.at[j, p]).wait()
+        low, count = passes[0] * PASS_ROWS, len(passes) * PASS_ROWS
 
         def o_step(c, _):
             cols = pl.ds(pl.multiple_of(c * CHUNK, CHUNK), CHUNK)
-            y = jnp.dot(mixed[j], wobuf[:, cols], preferred_element_type=F32)
-            part[...] = y
-            osend[j, :, cols] = y.astype(BF16)
-
-            def rows_of(index):
-                return pl.ds(pl.multiple_of(index * out_rows, out_rows), out_rows)
-
-            oself[j, :, cols] = part[rows_of(t), :]
-            for d in (2, 1, 3):
-                peer = lax.rem(t + d, TENSOR)
-                pltpu.make_async_remote_copy(
-                    src_ref=osend.at[j, rows_of(peer), cols], dst_ref=orecv.at[j, d - 1, :, cols],
-                    send_sem=o_send_sem.at[j, d - 1], recv_sem=o_sem.at[j, d - 1],
-                    device_id={"tensor": peer}, device_id_type=MESH).start()
+            y = jnp.dot(mixed[j, low:low + count], wobuf[:, cols], preferred_element_type=F32)
+            part[0:count] = y
+            osend[j, low:low + count, cols] = y.astype(BF16)
+            for p in passes:
+                def rows_of(index, base):
+                    return pl.ds(pl.multiple_of(p * PASS_ROWS - base + index * PASS_TOKENS, PASS_TOKENS), PASS_TOKENS)
+
+                place = slice(p * PASS_TOKENS, (p + 1) * PASS_TOKENS)
+                oself[j, place, cols] = part[rows_of(t, low), :]
+                for d in (2, 1, 3):
+                    peer = lax.rem(t + d, TENSOR)
+                    pltpu.make_async_remote_copy(
+                        src_ref=osend.at[j, rows_of(peer, 0), cols], dst_ref=orecv.at[j, d - 1, place, cols],
+                        send_sem=o_send_sem.at[j, d - 1], recv_sem=o_sem.at[j, d - 1],
+                        device_id={"tensor": peer}, device_id_type=MESH).start()
             return 0
 
         lax.fori_loop(0, D // CHUNK, o_step, 0)
@@ -323,8 +342,9 @@
         for mat in range(3):
             left = send.at[mat, pl.ds(0, 4 * TILES - 1)]
             pltpu.make_async_copy(left, left, send_sem.at[mat]).wait()
-        left = amix.at[pl.ds(0, SEQ_DEV - 1)]
-        pltpu.make_async_copy(left, left, mix_send_sem).wait()
+        for p in range(PASSES):
+            left = amix.at[p, pl.ds(0, SEQ_DEV - 1)]
+            pltpu.make_async_copy(left, left, mix_send_sem.at[p]).wait()
 
     @pl.when(jnp.logical_not(attends))
     def _():
@@ -360,7 +380,7 @@
             pltpu.VMEM((2, PAIR_ROWS, LOCAL), F32),
             pltpu.VMEM((3, 4 * TILES, ROWS, 128), BF16),
             pltpu.VMEM((3, SEQ_DEV, ROWS, 128), BF16),
-            pltpu.VMEM((SEQ_DEV, ROWS, 128), BF16),
+            pltpu.VMEM((PASSES, SEQ_DEV, PASS_ROWS, 128), BF16),
             pltpu.VMEM((2, ROWS, LOCAL), BF16),
             pltpu.VMEM((ROWS, CHUNK), F32),
             pltpu.VMEM((2, ROWS, D), BF16),
@@ -369,7 +389,7 @@
             pltpu.VMEM((2, 8, PAIR_ROWS), F32),
             pltpu.VMEM((2, TENSOR - 1, 8, PAIR_ROWS), F32),
             pltpu.VMEM((2, PAIR_ROWS, HEAD_DIM), F32),
-            dma, dma((3,)), dma((SLOTS,)), dma, dma((3,)), dma((3,)), dma, dma((2,)),
+            dma, dma((3,)), dma((SLOTS,)), dma, dma((3,)), dma((3,)), dma((PASSES,)), dma((2, PASSES)),
             dma((2, TENSOR - 1)), dma((2, TENSOR - 1)), dma((2, TENSOR - 1)), dma((2, TENSOR - 1)),
         ],
         compiler_params=pltpu.CompilerParams(

time: 66.9 us -> 68.1 us (1.018)
  Pallas kernels: 66.7 us -> 67.5 us
    pallas_call x1, Pallas kernels: 65 us -> 65.7 us  [local(): pl.pallas_call(kernel, out_shape=jax.ShapeDtypeStruct((ROWS // TENSOR, 2,...]
where the time goes in v5:
time: 68.1 us; the launch traced here: 67.5 us
  Pallas kernels  67.5 us (99%)
    pallas_call x1, Pallas kernels, local(): pl.pallas_call(kernel, out_shape=jax.ShapeDtypeStruct((ROWS // TENSOR, 2,...  65.7 us
    pallas_call x1, Pallas kernels, local(): pl.pallas_call(write_out, out_shape=jax.ShapeDtypeStruct(out.shape, BF16)...  1.72 us

profile of v5, /device:TPU:192, one launch (start us, length us, event | category | flops | bytes accessed | tf_op | source)
XLA Modules:
  0.0 67.5 jit_solution(8317823963129110929)
XLA Ops:
  0.0 65.7 %layer.1.y_ref = bf16[16,2,5120]{2,1,0:T(2,128)(2,1)} custom-call(bf16[64,2,5120]{2,1,0:T(2,128)(2,1)} %tok_hbm.1, f32[1280]{0:T(1024)} %gq_hbm.1, f32[1280]{0:T(1024)} %gk_hbm.1, f32[1,128]{1,0:T(1,128)} %constant.2.clone.freq_hbm, bf16[5120,1280]{1,0:T(8,128)(2,1)} %wq_hbm.1, bf16[5120,1280]{1,0:T(8,128)(2,1)} %wk_hbm.1, bf16[5120,1280]{1,0:T(8,128)(2,1)} %wv_hbm.1, ...), custom_call_target="tpu_custom_call" | custom-call | tf_op jit(solution)/shard_map/layer/pallas_call | solution.py:367
  65.8 1.7 %write_out.1 = bf16[16,2,5120]{2,1,0:T(2,128)(2,1)} custom-call(bf16[16,2,5120]{2,1,0:T(2,128)(2,1)} %layer.1.y_ref), custom_call_target="tpu_custom_call" | custom-call | tf_op jit(solution)/shard_map/write_out/pallas_call | solution.py:399
